TPU v7x, 32 devices: a whole 2x2x4 slice. The times are simulated.
32 devices in a mesh: heads: 4 (over y, core), batch: 8 (over z, x).
Axes of the slice: x: 2, y: 2, z: 4, core: 2. Of those that a mesh axis runs over, the one named last changes fastest.
Arguments:
- queries: bfloat16 [64, 4096], P('batch', 'heads'), may hold values from -6 to 6
- keys_new: bfloat16 [64, 4096], P('batch', 'heads'), may hold values from -6 to 6
- values_new: bfloat16 [64, 4096], P('batch', 'heads'), may hold values from -6 to 6
- out_gate: bfloat16 [64, 4096], P('batch', 'heads'), may hold values from -6 to 6
- decay_logit: float32 [64, 32], P('batch', 'heads'), may hold values from -6 to 6
- beta_logit: float32 [64, 32], P('batch', 'heads'), may hold values from -6 to 6
- decay_rate: float32 [32], P('heads'), may hold values from 0.05 to 2
- state: float32 [64, 32, 128, 128], P('batch', 'heads'), may hold values from -0.6 to 0.6
- norm_gain: float32 [128], replicated, may hold values from 0.1 to 1.9
- out_proj: bfloat16 [4096, 4096], P('heads'), may hold values from -0.09375 to 0.09375
- residual: bfloat16 [64, 4096], P('batch'), may hold values from -40 to 40, as said below
- final_gain: float32 [4096], replicated, may hold values from 0.1 to 1.9
- value_weight: float32 [4096], replicated, may hold values from -0.09375 to 0.09375
- lm_head: bfloat16 [4096, 4096], P(None, ('heads', 'batch')), may hold values from -15 to 15
- sampled: int32 [64], replicated, may hold values from 0 to 4095
Outputs:
- logprob: float32 [64], P('batch')
- value: float32 [64], P('batch')
Inputs may be any that keep to these rules, and one draw needn't show every extreme that they name: The residual stream's entries have scales that differ by row and by column (up to tenfold each), so neither rows nor columns share one magnitude.
All inputs are finite; a program needn't handle non-finite values.
Results may differ from a plain program's by a relative error of at most 0.0013.
Values may be sent and summed in bfloat16 or wider, within the bound.
A program may use at most 64 MiB of HBM per device.

v0:
```python
import jax
import jax.numpy as jnp
from jax import lax
from jax.sharding import PartitionSpec as P

epsilon = 1e-06


def joined(part, axis, combine):
    gathered = jax.tree.map(lambda a: lax.all_gather(a, axis), part)

    def take(source):
        return jax.tree.map(lambda a: lax.dynamic_index_in_dim(a, source, 0, False), gathered)

    return lax.fori_loop(
        1, lax.axis_size(axis), lambda source, state: combine(state, take(source)), take(0)
    )


def head_outputs(
    queries, keys_new, values_new, out_gate, decay_logit, beta_logit, decay_rate, state, norm_gain
):
    rows_here, heads_here = decay_logit.shape
    query_f = queries.astype(jnp.float32).reshape(rows_here, heads_here, -1)
    key_f = keys_new.astype(jnp.float32).reshape(rows_here, heads_here, -1)
    value_f = values_new.astype(jnp.float32).reshape(rows_here, heads_here, -1)
    gate_f = out_gate.astype(jnp.float32).reshape(rows_here, heads_here, -1)
    key_size = query_f.shape[2]
    query_n = query_f / jnp.sqrt(jnp.sum(query_f * query_f, axis=2, keepdims=True) + epsilon)
    query_n = query_n * key_size ** (-0.5)
    key_n = key_f / jnp.sqrt(jnp.sum(key_f * key_f, axis=2, keepdims=True) + epsilon)
    decay = jnp.exp(-decay_rate[None, :] * jax.nn.softplus(decay_logit))
    strength = jax.nn.sigmoid(beta_logit)
    state_query = jnp.einsum("bhk,bhkv->bhv", query_n, state, precision=lax.Precision.HIGHEST)
    state_key = jnp.einsum("bhk,bhkv->bhv", key_n, state, precision=lax.Precision.HIGHEST)
    intersection = jnp.sum(query_n * key_n, axis=2, keepdims=True)
    written = value_f - decay[..., None] * state_key
    output = decay[..., None] * state_query + strength[..., None] * intersection * written
    normed = output / jnp.sqrt(jnp.mean(output * output, axis=2, keepdims=True) + epsilon)
    result = normed * norm_gain * jax.nn.silu(gate_f)
    return result.reshape(rows_here, -1).astype(jnp.bfloat16)


def merge_stats(earlier, later):
    top = jnp.maximum(earlier[0], later[0])
    total = earlier[1] * jnp.exp(earlier[0] - top) + later[1] * jnp.exp(later[0] - top)
    return (top, total, earlier[2] + later[2])


def per_device(
    queries,
    keys_new,
    values_new,
    out_gate,
    decay_logit,
    beta_logit,
    decay_rate,
    state,
    norm_gain,
    out_proj,
    residual,
    final_gain,
    value_weight,
    lm_head,
    sampled,
):
    headout = head_outputs(
        queries,
        keys_new,
        values_new,
        out_gate,
        decay_logit,
        beta_logit,
        decay_rate,
        state,
        norm_gain,
    )
    partial_out = jnp.dot(headout, out_proj, preferred_element_type=jnp.float32)
    rows_own = residual.shape[0]
    attn = lax.psum(partial_out, "heads")
    hsum = residual.astype(jnp.float32) + attn
    rstd = 1.0 / jnp.sqrt(jnp.mean(hsum * hsum, axis=1) + epsilon)
    value = rstd * jnp.sum(hsum * final_gain * value_weight, axis=1)
    normed = (hsum * rstd[:, None] * final_gain).astype(jnp.bfloat16)
    logits = jnp.dot(
        lax.all_gather(normed, "batch", axis=0, tiled=True),
        lm_head,
        preferred_element_type=jnp.float32,
    )
    vocab_own = lm_head.shape[1]
    vocab_first = lax.axis_index(("heads", "batch")) * vocab_own
    local_ids = sampled - vocab_first
    columns = lax.broadcasted_iota(jnp.int32, logits.shape, 1)
    chosen = jnp.sum(jnp.where(columns == local_ids[:, None], logits, 0.0), axis=1)
    local_top = jnp.max(logits, axis=1)
    local_total = jnp.sum(jnp.exp(logits - local_top[:, None]), axis=1)
    top, total, chosen_all = joined(
        (local_top, local_total, chosen), ("heads", "batch"), merge_stats
    )
    every_logprob = chosen_all - (top + jnp.log(total))
    logprob = lax.dynamic_slice_in_dim(
        every_logprob, lax.axis_index("batch") * rows_own, rows_own, 0
    )
    return (logprob, value)


def solution(mesh):
    placed = (
        P("batch", "heads"),
        P("batch", "heads"),
        P("batch", "heads"),
        P("batch", "heads"),
        P("batch", "heads"),
        P("batch", "heads"),
        P("heads"),
        P("batch", "heads", None, None),
        P(),
        P("heads", None),
        P("batch", None),
        P(),
        P(),
        P(None, ("heads", "batch")),
        P(),
    )
    return jax.shard_map(
        per_device, mesh=mesh, in_specs=placed, out_specs=(P("batch"), P("batch")), check_vma=False
    )
```

profile of v0, /device:TPU:0, one launch (start us, length us, event | category | flops | bytes accessed | tf_op | source)
XLA Modules:
  0.0 143.0 jit_solution(5027682328408560421)
XLA Ops:
  7.2 0.0 copy-start
  7.2 0.0 all-reduce.6.cloned.1.call-start
  7.2 0.0 copy-start.1
  7.2 1.0 fusion.7
  8.2 1.1 fusion.9
  9.3 0.9 fusion.22
  10.2 0.0 copy-start.7
  10.3 0.0 copy-start.10
  10.3 0.0 copy-start.8
  10.3 0.0 copy-start.3
  10.3 0.0 copy-start.5
  10.3 0.0 copy-start.9
  10.3 5.3 %fusion.16 = f32[8,8,1,128]{3,2,1,0:T(1,128)S(1)} fusion(f32[8,8,128,128]{3,2,1,0:T(8,128)} %param.24, f32[8,8,128,1]{2,0,1,3:T(8,128)S(1)} %get-tuple-element.209), kind=kOutput, calls=%fused_computation.32 | convolution fusion | flops 12582912 | bytes 4259840 | tf_op jit(solution)/shard_map/bhk,bhkv->bhv/dot_general | solution.py:35
  15.6 0.0 copy-done.1
  15.6 3.7 %fusion.18 = f32[8,8,1,128]{3,2,1,0:T(1,128)S(1)} fusion(f32[8,8,128,128]{3,2,1,0:T(8,128)S(1)} %copy-done.1, f32[8,8,128,1]{2,0,1,3:T(8,128)S(1)} %get-tuple-element.207), kind=kOutput, calls=%fused_computation.34 | convolution fusion | flops 12582912 | bytes 4259840 | tf_op jit(solution)/shard_map/bhk,bhkv->bhv/dot_general | solution.py:34
  19.3 0.0 copy-done.7
  19.3 0.1 copy.20
  19.4 0.0 copy-done.10
  19.4 0.0 copy-done.8
  19.4 0.1 copy.19
  19.5 0.2 multiply_reduce_fusion.2
  19.7 0.0 copy-done.5
  19.7 0.0 copy-done.9
  19.7 0.0 copy-start.11
  19.7 0.0 copy-start.2
  19.7 0.0 copy-start.4
  19.7 0.0 copy-start.6
  19.7 5.3 %fusion.23 = f32[8,4096]{1,0:T(8,128)} fusion(bf16[1024,4096]{1,0:T(8,128)(2,1)} %param.26, bf16[8,1024]{1,0:T(8,128)(2,1)S(1)} %copy-done.5, f32[128]{0:T(128)S(1)} %copy-done.9, f32[8,8]{0,1:T(8,128)S(1)} %add_sqrt_fusion, f32[8,8,1,128]{3,2,1,0:T(1,128)S(1)} %fusion.16, f32[8,8,1,128]{3,2,1,0:T(1,128)S(1)} %fusion.18, bf16[8,1024]{1,0:T(8,128)(2,1)S(1)} %copy-done.3, ...), kind=kOutput, calls=%fused_computation.44 | convolution fusion | flops 67231744 | bytes 8619264 | tf_op jit(solution)/shard_map/dot_general | solution.py:78
  25.0 0.0 all-reduce.6.cloned.1.call-update
  25.1 34.6 %all-reduce.6.cloned.1.call-done = f32[8,4096]{1,0:T(8,128)} async-done(((f32[8,4096]{1,0:T(8,128)}), f32[8,4096]{1,0:T(8,128)}) %all-reduce.6.cloned.1.call-update) | async-done | bytes 131088 | tf_op jit(solution)/shard_map/psum | solution.py:80
  59.7 0.0 copy-done.2
  59.7 0.0 copy-done.6
  59.7 1.1 multiply_reduce_fusion
  60.8 0.5 fusion.32
  61.4 1.0 multiply_convert_fusion
  62.4 31.4 %all_gather.21 = bf16[64,4096]{1,0:T(8,128)(2,1)S(1)} all-gather(bf16[8,4096]{1,0:T(8,128)(2,1)S(1)} %multiply_convert_fusion), channel_id=1, replica_groups=mesh['heads'=4,'batch'=8] {'batch'}, dimensions={0}, use_global_device_ids=true | all-gather | bytes 589824 | tf_op jit(solution)/shard_map/all_gather | solution.py:86
  93.7 0.0 copy-done
  93.7 0.4 fusion.35
  94.2 0.2 select_reduce_fusion
  94.4 0.3 dynamic-update-slice
  94.7 0.3 dynamic-update-slice.2
  94.9 0.3 dynamic-update-slice.1
  95.2 38.7 %all-reduce.3 = (f32[2048]{0:T(1024)S(1)}, f32[2048]{0:T(1024)S(1)}, f32[2048]{0:T(1024)S(1)}) all-reduce(f32[2048]{0:T(1024)S(1)} %dynamic-update-slice, f32[2048]{0:T(1024)S(1)} %dynamic-update-slice.1, f32[2048]{0:T(1024)S(1)} %dynamic-update-slice.2), channel_id=2, replica_groups=mesh['heads'=4,'batch'=8] {'heads','batch'}, use_global_device_ids=true, to_apply=%add | all-reduce | flops 6144 | bytes 49152
  133.8 0.1 reshape.81
  133.9 0.1 reshape.82
  134.0 0.1 reshape.83
  134.1 1.4 %while.19 = (s32[]{:T(128)}, f32[64]{0:T(128)S(1)}, f32[64]{0:T(128)S(1)}, f32[64]{0:T(128)S(1)}, f32[32,64]{1,0:T(8,128)S(1)}, /*index=5*/f32[32,64]{1,0:T(8,12...) while((s32[]{:T(128)}, f32[64]{0:T(128)S(1)}, f32[64]{0:T(128)S(1)}, f32[64]{0:T(128)S(1)}, ...), condition=%wide.region_10.11_spmd, body=%wide.region_9.10_spmd.sunk | while | flops 453 | bytes 2451 | solution.py:15
  135.5 0.6 dynamic_slice.46
  (47 shorter events, 1.0 us)
Async XLA Ops:
  7.2 86.6 %copy-start = (bf16[4096,128]{1,0:T(8,128)(2,1)S(1)}, bf16[4096,128]{1,0:T(8,128)(2,1)}, u32[]{:S(2)}) copy-start(bf16[4096,128]{1,0:T(8,128)(2,1)} %param.30) | copy-start | bytes 3145732
  7.2 52.6 %all-reduce.6.cloned.1.call-start = ((), (), s32[]{:S(2)}) async-start(), calls=%async_computation | async-start | bytes 262144 | tf_op jit(solution)/shard_map/psum | solution.py:80
  7.2 8.4 %copy-start.1 = (f32[8,8,128,128]{3,2,1,0:T(8,128)S(1)}, f32[8,8,128,128]{3,2,1,0:T(8,128)}, u32[]{:S(2)}) copy-start(f32[8,8,128,128]{3,2,1,0:T(8,128)} %param.24) | copy-start | bytes 12582916
  10.2 9.1 %copy-start.7 = (f32[8,8]{1,0:T(8,128)S(1)}, f32[8,8]{1,0:T(8,128)}, u32[]{:S(2)}) copy-start(f32[8,8]{1,0:T(8,128)} %param.22) | copy-start | bytes 772
  10.3 9.1 %copy-start.10 = (f32[8]{0:T(128)S(1)}, f32[8]{0:T(128)}, u32[]{:S(2)}) copy-start(f32[8]{0:T(128)} %param.23) | copy-start | bytes 100
  10.3 9.1 %copy-start.8 = (f32[8,8]{1,0:T(8,128)S(1)}, f32[8,8]{1,0:T(8,128)}, u32[]{:S(2)}) copy-start(f32[8,8]{1,0:T(8,128)} %param.21) | copy-start | bytes 772
  10.3 9.2 %copy-start.3 = (bf16[8,1024]{1,0:T(8,128)(2,1)S(1)}, bf16[8,1024]{1,0:T(8,128)(2,1)}, u32[]{:S(2)}) copy-start(bf16[8,1024]{1,0:T(8,128)(2,1)} %param.19) | copy-start | bytes 49156
  10.3 9.4 %copy-start.5 = (bf16[8,1024]{1,0:T(8,128)(2,1)S(1)}, bf16[8,1024]{1,0:T(8,128)(2,1)}, u32[]{:S(2)}) copy-start(bf16[8,1024]{1,0:T(8,128)(2,1)} %param.20) | copy-start | bytes 49156
  10.3 9.4 %copy-start.9 = (f32[128]{0:T(128)S(1)}, f32[128]{0:T(128)}, u32[]{:S(2)}) copy-start(f32[128]{0:T(128)} %param.25) | copy-start | bytes 1540
  19.7 5.4 %copy-start.11 = (s32[64]{0:T(128)S(1)}, s32[64]{0:T(128)}, u32[]{:S(2)}) copy-start(s32[64]{0:T(128)} %param.31) | copy-start | bytes 772
  19.7 40.0 %copy-start.2 = (bf16[8,4096]{1,0:T(8,128)(2,1)S(1)}, bf16[8,4096]{1,0:T(8,128)(2,1)}, u32[]{:S(2)}) copy-start(bf16[8,4096]{1,0:T(8,128)(2,1)} %param.27) | copy-start | bytes 196612
  19.7 40.0 %copy-start.4 = (f32[4096]{0:T(1024)S(1)}, f32[4096]{0:T(1024)}, u32[]{:S(2)}) copy-start(f32[4096]{0:T(1024)} %param.28) | copy-start | bytes 49156
  19.7 40.0 %copy-start.6 = (f32[4096]{0:T(1024)S(1)}, f32[4096]{0:T(1024)}, u32[]{:S(2)}) copy-start(f32[4096]{0:T(1024)} %param.29) | copy-start | bytes 49156
Sparse Core Ops, SparseCore 0:
  25.2 34.4 all-reduce.5
where the time goes:
time: 144 us; the launch traced here: 143 us
  blocking collectives  70.1 us (49%)
  waiting for transfers between devices  34.6 us (24%)
  matrix products  14.7 us (10%)
  between operations  14.2 us (10%)
  other arithmetic  6.89 us (5%)
  local copies, waits for them, and re-layouts  1.82 us (1%)
    unnamed x1, blocking collectives  38.7 us
    psum x1, waiting for transfers between devices, per_device(): attn = lax.psum(partial_out, 'heads')  34.6 us
    all_gather x1, blocking collectives, per_device(): lax.all_gather(normed, 'batch', axis=0, tiled=True)  31.4 us
    dot_general x1, matrix products, head_outputs(): jnp.einsum('bhk,bhkv->bhv', key_n, state, precision=lax.Precision.HIGHEST)  5.31 us
    dot_general x1, matrix products, per_device(): partial_out = jnp.dot(headout, out_proj, preferred_element_type=jnp.float32)  5.31 us
    dot_general x1, matrix products, head_outputs(): jnp.einsum('bhk,bhkv->bhv', query_n, state, precision=lax.Precision.HIGHEST)  3.66 us
  transfers between devices with their start and end apart: 1, of which 1 were waited for; matrix products, arithmetic and copies ran while one was open for 0% of the time, Pallas kernels for 0%

commit v1 on v0

--- a/solution.py
+++ b/solution.py
@@ -1,9 +1,22 @@
+import functools
 import jax
 import jax.numpy as jnp
 from jax import lax
 from jax.sharding import PartitionSpec as P
 
 epsilon = 1e-06
+
+
+def advance_pages_in(x_in, a_name):
+    clean = x_in
+    devs = lax.axis_size(a_name)
+    for u in [[(i0, i0 ^ i) for i0 in range(devs)] for i in (1, 2, 4, 8, 16) if i < devs]:
+        frame_out = lax.ppermute(clean, a_name, u)
+        clean = clean + frame_out
+    return clean
+
+
+_do_targets = functools.partial(advance_pages_in, a_name="heads")
 
 
 def joined(part, axis, combine):
@@ -77,7 +90,7 @@
     )
     partial_out = jnp.dot(headout, out_proj, preferred_element_type=jnp.float32)
     rows_own = residual.shape[0]
-    attn = lax.psum(partial_out, "heads")
+    attn = _do_targets(partial_out)
     hsum = residual.astype(jnp.float32) + attn
     rstd = 1.0 / jnp.sqrt(jnp.mean(hsum * hsum, axis=1) + epsilon)
     value = rstd * jnp.sum(hsum * final_gain * value_weight, axis=1)

time: 144 us -> 103 us (0.72)
  waiting for transfers between devices: 34.6 us -> 4.79 us
  between operations: 14.2 us -> 0.83 us
  starting transfers between devices: 0.04 us -> 3.43 us
  other arithmetic: 6.89 us -> 5.12 us
    psum x1 -> x0, waiting for transfers between devices: 34.6 us -> none  [per_device(): attn = lax.psum(partial_out, 'heads')]
    ppermute x0 -> x2, waiting for transfers between devices: none -> 4.79 us  [advance_pages_in(): frame_out = lax.ppermute(clean, a_name, u)]
    ppermute x0 -> x2, starting transfers between devices: none -> 3.43 us  [advance_pages_in(): frame_out = lax.ppermute(clean, a_name, u)]
  transfers between devices with their start and end apart: 1 -> 2, of which waited for: 1 -> 2; matrix products, arithmetic and copies ran while one was open for 0% -> 0% of each run, Pallas kernels for 0% -> 0%
where the time goes in v1:
time: 103 us; the launch traced here: 102 us
  blocking collectives  71.5 us (69%)
  matrix products  14 us (14%)
  other arithmetic  5.12 us (5%)
  waiting for transfers between devices  4.79 us (5%)
  starting transfers between devices  3.43 us (3%)
  local copies, waits for them, and re-layouts  1.82 us (2%)
    unnamed x1, blocking collectives  39.5 us
    all_gather x1, blocking collectives, per_device(): lax.all_gather(normed, 'batch', axis=0, tiled=True)  32 us
    dot_general x1, matrix products, head_outputs(): jnp.einsum('bhk,bhkv->bhv', key_n, state, precision=lax.Precision.HIGHEST)  5.31 us
    ppermute x2, waiting for transfers between devices, advance_pages_in(): frame_out = lax.ppermute(clean, a_name, u)  4.79 us
    dot_general x1, matrix products, per_device(): partial_out = jnp.dot(headout, out_proj, preferred_element_type=jnp.float32)  4.65 us
    dot_general x1, matrix products, head_outputs(): jnp.einsum('bhk,bhkv->bhv', query_n, state, precision=lax.Precision.HIGHEST)  3.66 us
    ppermute x2, starting transfers between devices, advance_pages_in(): frame_out = lax.ppermute(clean, a_name, u)  3.43 us
  transfers between devices with their start and end apart: 2, of which 2 were waited for; matrix products, arithmetic and copies ran while one was open for 0% of the time, Pallas kernels for 0%

profile of v1, /device:TPU:0, one launch (start us, length us, event | category | flops | bytes accessed | tf_op | source)
XLA Modules:
  0.0 102.1 jit_solution(7401566609361369546)
XLA Ops:
  0.6 0.0 copy-start
  0.6 0.0 copy-start.1
  0.7 1.0 fusion.7
  1.6 1.1 %fusion.9 = f32[8,8]{0,1:T(8,128)S(1)} fusion(bf16[8,1024]{1,0:T(8,128)(2,1)} %param.18), kind=kLoop, calls=%fused_computation.22 | loop fusion | flops 24512 | bytes 16640 | tf_op jit(solution)/shard_map/reduce_sum | solution.py:44
  2.8 0.9 fusion.22
  3.7 0.0 copy-start.7
  3.7 0.0 copy-start.10
  3.7 0.0 copy-start.8
  3.7 0.0 copy-start.2
  3.7 0.0 copy-start.5
  3.7 0.0 copy-start.9
  3.7 5.3 %fusion.16 = f32[8,8,1,128]{3,2,1,0:T(1,128)S(1)} fusion(f32[8,8,128,128]{3,2,1,0:T(8,128)} %param.24, f32[8,8,128,1]{2,0,1,3:T(8,128)S(1)} %get-tuple-element.210), kind=kOutput, calls=%fused_computation.32 | convolution fusion | flops 12582912 | bytes 4259840 | tf_op jit(solution)/shard_map/bhk,bhkv->bhv/dot_general | solution.py:48
  9.1 0.0 copy-done.1
  9.1 3.7 %fusion.18 = f32[8,8,1,128]{3,2,1,0:T(1,128)S(1)} fusion(f32[8,8,128,128]{3,2,1,0:T(8,128)S(1)} %copy-done.1, f32[8,8,128,1]{2,0,1,3:T(8,128)S(1)} %get-tuple-element.208), kind=kOutput, calls=%fused_computation.34 | convolution fusion | flops 12582912 | bytes 4259840 | tf_op jit(solution)/shard_map/bhk,bhkv->bhv/dot_general | solution.py:47
  12.7 0.0 copy-done.7
  12.7 0.1 copy.20
  12.8 0.0 copy-done.10
  12.8 0.0 copy-done.8
  12.8 0.1 copy.19
  12.9 0.0 copy-done.2
  12.9 0.2 multiply_reduce_fusion.2
  13.1 0.0 copy-done.5
  13.1 0.0 copy-start.11
  13.1 0.0 copy-start.3
  13.1 0.0 copy-start.4
  13.2 0.0 copy-start.6
  13.2 4.6 %fusion.23 = f32[8,4096]{1,0:T(8,128)S(1)} fusion(bf16[1024,4096]{1,0:T(8,128)(2,1)} %param.26, bf16[8,1024]{1,0:T(8,128)(2,1)S(1)} %copy-done.5, f32[128]{0:T(128)S(1)} %copy-done.9, f32[8,8]{0,1:T(8,128)S(1)} %add_sqrt_fusion, f32[8,8,1,128]{3,2,1,0:T(1,128)S(1)} %fusion.16, f32[8,8,1,128]{3,2,1,0:T(1,128)S(1)} %fusion.18, ...), kind=kOutput, calls=%fused_computation.44 | convolution fusion | flops 67231744 | bytes 8619264 | tf_op jit(solution)/shard_map/dot_general | solution.py:91
  17.8 0.5 collective-permute-start
  18.3 1.0 collective-permute-done
  19.3 2.9 %collective-permute-start.1 = (f32[8,4096]{1,0:T(8,128)S(1)}, f32[8,4096]{1,0:T(8,128)S(1)}, u32[]{:S(2)}, u32[]{:S(2)}) collective-permute-start(f32[8,4096]{1,0:T(8,128)S(1)} %add.129), channel_id=1, source_target_pairs={{0,16},{8,24},{16,0},{24,8},{1,17},{9,25},{17,1},{25,9},{2,18},{10... | collective-permute-start | bytes 393224 | tf_op jit(solution)/shard_map/ppermute | solution.py:14
  22.3 0.0 copy-done.11
  22.3 3.8 %collective-permute-done.1 = f32[8,4096]{1,0:T(8,128)S(1)} collective-permute-done((f32[8,4096]{1,0:T(8,128)S(1)}, f32[8,4096]{1,0:T(8,128)S(1)}, u32[]{:S(2)}, u32[]{:S(2)}) %collective-permute-start.1) | collective-permute-done | bytes 131104 | tf_op jit(solution)/shard_map/ppermute | solution.py:14
  26.1 0.0 copy-done.3
  26.1 0.2 multiply_reduce_fusion
  26.3 0.5 fusion.32
  26.8 0.1 multiply_convert_fusion
  26.9 32.0 %all_gather.21 = bf16[64,4096]{1,0:T(8,128)(2,1)S(1)} all-gather(bf16[8,4096]{1,0:T(8,128)(2,1)S(1)} %multiply_convert_fusion), channel_id=1, replica_groups=mesh['heads'=4,'batch'=8] {'batch'}, dimensions={0}, use_global_device_ids=true | all-gather | bytes 589824 | tf_op jit(solution)/shard_map/all_gather | solution.py:99
  58.9 0.4 fusion.35
  59.3 0.2 select_reduce_fusion
  59.5 0.3 dynamic-update-slice
  59.8 0.3 dynamic-update-slice.2
  60.0 0.3 dynamic-update-slice.1
  60.3 39.5 %all-reduce.3 = (f32[2048]{0:T(1024)S(1)}, f32[2048]{0:T(1024)S(1)}, f32[2048]{0:T(1024)S(1)}) all-reduce(f32[2048]{0:T(1024)S(1)} %dynamic-update-slice, f32[2048]{0:T(1024)S(1)} %dynamic-update-slice.1, f32[2048]{0:T(1024)S(1)} %dynamic-update-slice.2), channel_id=2, replica_groups=mesh['heads'=4,'batch'=8] {'heads','batch'}, use_global_device_ids=true, to_apply=%add | all-reduce | flops 6144 | bytes 49152
  99.8 0.1 reshape.81
  99.9 0.1 reshape.82
  100.0 0.1 reshape.83
  100.1 1.4 %while.19 = (s32[]{:T(128)}, f32[64]{0:T(128)S(1)}, f32[64]{0:T(128)S(1)}, f32[64]{0:T(128)S(1)}, f32[32,64]{1,0:T(8,128)S(1)}, /*index=5*/f32[32,64]{1,0:T(8,12...) while((s32[]{:T(128)}, f32[64]{0:T(128)S(1)}, f32[64]{0:T(128)S(1)}, f32[64]{0:T(128)S(1)}, ...), condition=%wide.region_9.10_spmd, body=%wide.region_8.9_spmd.sunk | while | flops 453 | bytes 2451 | solution.py:28
  101.5 0.6 dynamic_slice.46
  (49 shorter events, 1.0 us)
Async XLA Ops:
  0.6 58.2 %copy-start = (bf16[4096,128]{1,0:T(8,128)(2,1)S(1)}, bf16[4096,128]{1,0:T(8,128)(2,1)}, u32[]{:S(2)}) copy-start(bf16[4096,128]{1,0:T(8,128)(2,1)} %param.30) | copy-start | bytes 3145732
  0.6 8.4 %copy-start.1 = (f32[8,8,128,128]{3,2,1,0:T(8,128)S(1)}, f32[8,8,128,128]{3,2,1,0:T(8,128)}, u32[]{:S(2)}) copy-start(f32[8,8,128,128]{3,2,1,0:T(8,128)} %param.24) | copy-start | bytes 12582916
  3.7 9.1 %copy-start.7 = (f32[8,8]{1,0:T(8,128)S(1)}, f32[8,8]{1,0:T(8,128)}, u32[]{:S(2)}) copy-start(f32[8,8]{1,0:T(8,128)} %param.22) | copy-start | bytes 772
  3.7 9.1 %copy-start.10 = (f32[8]{0:T(128)S(1)}, f32[8]{0:T(128)}, u32[]{:S(2)}) copy-start(f32[8]{0:T(128)} %param.23) | copy-start | bytes 100
  3.7 9.1 %copy-start.8 = (f32[8,8]{1,0:T(8,128)S(1)}, f32[8,8]{1,0:T(8,128)}, u32[]{:S(2)}) copy-start(f32[8,8]{1,0:T(8,128)} %param.21) | copy-start | bytes 772
  3.7 9.2 %copy-start.2 = (bf16[8,1024]{1,0:T(8,128)(2,1)S(1)}, bf16[8,1024]{1,0:T(8,128)(2,1)}, u32[]{:S(2)}) copy-start(bf16[8,1024]{1,0:T(8,128)(2,1)} %param.19) | copy-start | bytes 49156
  3.7 9.4 %copy-start.5 = (bf16[8,1024]{1,0:T(8,128)(2,1)S(1)}, bf16[8,1024]{1,0:T(8,128)(2,1)}, u32[]{:S(2)}) copy-start(bf16[8,1024]{1,0:T(8,128)(2,1)} %param.20) | copy-start | bytes 49156
  3.7 9.4 %copy-start.9 = (f32[128]{0:T(128)S(1)}, f32[128]{0:T(128)}, u32[]{:S(2)}) copy-start(f32[128]{0:T(128)} %param.25) | copy-start | bytes 1540
  13.1 9.1 %copy-start.11 = (s32[64]{0:T(128)S(1)}, s32[64]{0:T(128)}, u32[]{:S(2)}) copy-start(s32[64]{0:T(128)} %param.31) | copy-start | bytes 772
  13.1 12.9 %copy-start.3 = (bf16[8,4096]{1,0:T(8,128)(2,1)S(1)}, bf16[8,4096]{1,0:T(8,128)(2,1)}, u32[]{:S(2)}) copy-start(bf16[8,4096]{1,0:T(8,128)(2,1)} %param.27) | copy-start | bytes 196612
  13.1 12.9 %copy-start.4 = (f32[4096]{0:T(1024)S(1)}, f32[4096]{0:T(1024)}, u32[]{:S(2)}) copy-start(f32[4096]{0:T(1024)} %param.28) | copy-start | bytes 49156
  13.2 12.9 %copy-start.6 = (f32[4096]{0:T(1024)S(1)}, f32[4096]{0:T(1024)}, u32[]{:S(2)}) copy-start(f32[4096]{0:T(1024)} %param.29) | copy-start | bytes 49156
  17.8 1.5 %collective-permute-start = (f32[8,4096]{1,0:T(8,128)S(1)}, f32[8,4096]{1,0:T(8,128)S(1)}, u32[]{:S(2)}, u32[]{:S(2)}) collective-permute-start(f32[8,4096]{1,0:T(8,128)S(1)} %fusion.23), channel_id=1, source_target_pairs={{0,8},{8,0},{16,24},{24,16},{1,9},{9,1},{17,25},{25,17},{2,10},{10... | collective-permute-start | bytes 393224 | tf_op jit(solution)/shard_map/ppermute | solution.py:14
  19.3 6.7 %collective-permute-start.1 = (f32[8,4096]{1,0:T(8,128)S(1)}, f32[8,4096]{1,0:T(8,128)S(1)}, u32[]{:S(2)}, u32[]{:S(2)}) collective-permute-start(f32[8,4096]{1,0:T(8,128)S(1)} %add.129), channel_id=1, source_target_pairs={{0,16},{8,24},{16,0},{24,8},{1,17},{9,25},{17,1},{25,9},{2,18},{10... | collective-permute-start | bytes 393224 | tf_op jit(solution)/shard_map/ppermute | solution.py:14
